TPU v7x, 256 devices: a whole 4x4x8 slice. The times are simulated.
256 devices in a mesh: shuf: 64 (over y, z, core), rep: 4 (over x).
Axes of the slice: x: 4, y: 4, z: 8, core: 2. Of those that a mesh axis runs over, the one named last changes fastest.
Arguments:
- values: bfloat16 [524288, 1024], P('shuf', 'rep')
- subgroup: int32 [4096], P('shuf'), may hold values from 0 to 31
- owners: int32 [4096, 1], P('shuf'), may hold values from 0 to 63; in each aligned block of 64 rows (0 to 63, 64 to 127, ...) at most 2 rows name the same one
- col_gain: float32 [1024], P('rep'), may hold values from 0.5 to 1.5
- col_bias: float32 [1024], P('rep'), may hold values from -3 to 3
- out_weight: bfloat16 [1024, 1024], P('rep'), may hold values from -0.1875 to 0.1875
Outputs:
- projected: bfloat16 [524288, 1024], P(('shuf', 'rep'))
Inputs may be any that keep to these rules, and one draw needn't show every extreme that they name: `owners`: among the tiles of one index of shuf no owner is named more than 2 times, a bound that some block reaches.
All inputs are finite; a program needn't handle non-finite values.
Results may differ from a plain program's by a relative error of at most 0.015.
Values may be sent and summed in bfloat16 or wider, within the bound.
No kernel may reach another device: no remote copies, remote signals or barrier semaphores. Data moves between devices by JAX's collectives and lax.ppermute only.
A program may use at most 64 MiB of HBM per device.

v0:
```python
import math
import jax
import jax.numpy as jnp
from jax import lax
from jax.sharding import PartitionSpec as P

GRP_DEV = 32
PRIOR = 256


def from_everyone(value, axis):
    peers = lax.axis_size(axis)
    return lax.all_to_all(
        jnp.broadcast_to(value[None], (peers, *value.shape)), axis, 0, 0, tiled=True
    )


def over_copies(value, axis):
    everything = from_everyone(value, axis)
    return jnp.sum(everything, axis=0)


def in_one(arrays, axis):
    flat, at, done = (jnp.concatenate([a.reshape(-1) for a in arrays]), 0, [])
    so_far = over_copies(flat, axis)
    for a in arrays:
        done.append(so_far[at : at + a.size].reshape(a.shape))
        at += a.size
    return tuple(done)


def side_by_side(arrays, axis, split_dim, concat_dim, along):
    widths = [math.prod(a.shape[along:]) for a in arrays]
    both = jnp.concatenate(
        [a.reshape(*a.shape[:along], w) for a, w in zip(arrays, widths)], axis=along
    )
    result = lax.all_to_all(both, axis, split_axis=split_dim, concat_axis=concat_dim, tiled=True)
    pieces = jnp.split(result, [sum(widths[:k]) for k in range(1, len(widths))], axis=along)
    return tuple(
        (b.reshape(*result.shape[:along], *a.shape[along:]) for a, b in zip(arrays, pieces))
    )


def in_one_piece(arrays, axis, split_dim, concat_dim, along):
    ends, at = ([], 0)
    for a in arrays[:-1]:
        at += a.shape[along]
        ends.append(at)
    both = jnp.concatenate(arrays, axis=along)
    return tuple(
        jnp.split(
            lax.all_to_all(both, axis, split_axis=split_dim, concat_axis=concat_dim, tiled=True),
            ends,
            axis=along,
        )
    )


def joined_along(pieces, dim):
    lengths = list(pieces.shape[1:])
    lengths[dim] *= pieces.shape[0]
    return jnp.moveaxis(pieces, 0, dim).reshape(lengths)


def gathered_copies(value, axis, dim):
    return joined_along(from_everyone(value, axis), dim)


def moments(group_sum, group_sq, count, mean_all, square_all):
    weight = (count + float(PRIOR))[:, None]
    center = (group_sum + float(PRIOR) * mean_all) / weight
    second = (group_sq + float(PRIOR) * square_all) / weight
    return (center, lax.rsqrt(second - center * center + 1e-05))


def slot_places(target, capacity, peer_count):
    one_hot = (target[:, None] == jnp.arange(peer_count, dtype=jnp.int32)[None, :]).astype(
        jnp.int32
    )
    position = jnp.sum((jnp.cumsum(one_hot, axis=0) - one_hot) * one_hot, axis=1)
    return target * capacity + position


def on_device(values, subgroup, owners, col_gain, col_bias, out_weight):
    local_rows, local_cols = values.shape
    tile_count = subgroup.shape[0]
    tile_rows = local_rows // tile_count
    peer_count = lax.axis_size("shuf")
    shaped = values.reshape(tile_count, tile_rows, local_cols)
    widened = shaped.astype(jnp.float32)
    tile_sum = jnp.sum(widened, axis=1)
    tile_sq = jnp.sum(widened * widened, axis=1)
    col_sum, col_square = in_one((jnp.sum(tile_sum, axis=0), jnp.sum(tile_sq, axis=0)), "shuf")
    row_count = float(local_rows * peer_count)
    mean_all = col_sum / row_count
    square_all = col_square / row_count
    target = owners[:, 0]
    capacity = max(2, 2 * tile_count // peer_count)
    slot_index = slot_places(target, capacity, peer_count)
    packed = jnp.concatenate([tile_sum, tile_sq], axis=1)
    outgoing = (
        jnp.zeros((peer_count * capacity, 2 * local_cols), jnp.float32).at[slot_index].set(packed)
    )
    labels = (
        jnp.full((peer_count * capacity,), -1.0, jnp.float32)
        .at[slot_index]
        .set(subgroup.astype(jnp.float32))
    )
    arrived, arrived_labels = tuple(
        (
            part.astype(jnp.float32)
            for part in side_by_side(
                (outgoing.astype(jnp.bfloat16), labels.astype(jnp.bfloat16)), "shuf", 0, 0, 1
            )
        )
    )
    group_ids = arrived_labels.astype(jnp.int32)
    members = (group_ids[:, None] == jnp.arange(GRP_DEV, dtype=jnp.int32)[None, :]).astype(
        jnp.float32
    )
    group_sum = jnp.dot(members.T, arrived[:, :local_cols])
    group_sq = jnp.dot(members.T, arrived[:, local_cols:])
    count = float(tile_rows) * jnp.sum(members, axis=0)
    center, inverse = moments(group_sum, group_sq, count, mean_all, square_all)
    slot_center = jnp.dot(members, center)
    slot_inverse = jnp.dot(members, inverse)
    back_center, back_inverse = tuple(
        (
            part.astype(jnp.float32)
            for part in in_one_piece(
                (slot_center.astype(jnp.bfloat16), slot_inverse.astype(jnp.bfloat16)),
                "shuf",
                0,
                0,
                1,
            )
        )
    )
    tile_center = back_center[slot_index]
    tile_scale = back_inverse[slot_index] * col_gain
    scored = ((widened - tile_center[:, None, :]) * tile_scale[:, None, :] + col_bias).astype(
        jnp.bfloat16
    )
    standard = scored.reshape(local_rows, local_cols)
    full_rows = lax.all_to_all(standard, "rep", split_axis=0, concat_axis=1, tiled=True)
    full_weight = gathered_copies(out_weight, "rep", 0)
    summed = jnp.zeros((full_rows.shape[0], full_weight.shape[1]), jnp.float32)
    for block in range(lax.axis_size("rep")):
        partial_value = jnp.dot(
            full_rows[:, block * local_cols : (block + 1) * local_cols],
            full_weight[block * local_cols : (block + 1) * local_cols],
            preferred_element_type=jnp.float32,
        )
        summed = summed + partial_value.astype(jnp.bfloat16).astype(jnp.float32)
    return summed.astype(jnp.bfloat16)


def solution(mesh):
    return jax.shard_map(
        on_device,
        mesh=mesh,
        in_specs=(P("shuf", "rep"), P("shuf"), P("shuf", None), P("rep"), P("rep"), P("rep", None)),
        out_specs=P(("shuf", "rep"), None),
        check_vma=False,
    )
```

profile of v0, /device:TPU:32, one launch (start us, length us, event | category | flops | bytes accessed | tf_op | source)
XLA Modules:
  0.0 160.4 jit_solution(14804359981047646363)
XLA Ops:
  0.0 0.0 copy-start.5
  0.0 0.0 copy-start.2
  0.0 3.3 %convert_reduce_fusion = (f32[256]{0:T(256)S(1)}, f32[256]{0:T(256)S(1)}) fusion(bf16[8192,256]{1,0:T(8,128)(2,1)} %param.6), kind=kLoop, calls=%fused_computation.11 | loop fusion | flops 8388096 | bytes 4196352 | tf_op jit(solution)/shard_map/reduce_sum | solution.py:93
  3.4 0.7 broadcast_in_dim.10
  4.1 11.8 %all-to-all-start.1 = ((f32[64,1,512]{2,1,0:T(1,128)}), f32[64,1,512]{2,1,0:T(1,128)S(1)}, u32[]{:S(2)}, u32[]{:S(2)}) async-start(f32[64,1,512]{2,1,0:T(1,128)} %broadcast_in_dim.10), calls=%async_computation.1 | async-start | bytes 262144 | tf_op jit(solution)/shard_map/all_to_all | solution.py:13
  15.8 0.0 copy-start.3
  15.8 0.0 copy-start.4
  15.9 4.6 %bitcast_reduce_fusion = (f32[64,256]{1,0:T(8,128)S(1)}, f32[64,256]{1,0:T(8,128)S(1)}) fusion(bf16[8192,256]{1,0:T(8,128)(2,1)} %param.6), kind=kLoop, calls=%fused_computation.9 | loop fusion | flops 8355840 | bytes 4325376 | tf_op jit(solution)/shard_map/reduce_sum | solution.py:91
  20.5 0.0 copy-done.5
  20.5 0.0 copy-done.2
  20.5 0.1 fusion.25
  20.6 0.1 reduce_window_sum.11
  20.7 0.2 select_reduce_fusion
  20.9 0.8 scatter_custom_fusion.1
  21.7 0.2 concatenate.23
  21.9 0.9 scatter_custom_fusion
  22.8 0.1 concatenate.18
  22.9 0.8 pad_maximum_fusion
  23.7 2.1 %all-to-all-done.1 = f32[64,1,512]{2,1,0:T(1,128)S(1)} async-done(((f32[64,1,512]{2,1,0:T(1,128)}), f32[64,1,512]{2,1,0:T(1,128)S(1)}, u32[]{:S(2)}, u32[]{:S(2)}) %all-to-all-start.1) | async-done | bytes 131104 | tf_op jit(solution)/shard_map/all_to_all | solution.py:13
  25.9 8.2 %all-to-all-start = ((bf16[64,2,513]{2,1,0:T(2,128)(2,1)}), bf16[64,2,513]{2,1,0:T(2,128)(2,1)S(1)}, u32[]{:S(2)}, u32[]{:S(2)}) async-start(bf16[64,2,513]{2,1,0:T(2,128)(2,1)} %pad_maximum_fusion), calls=%async_computation | async-start | bytes 327680 | tf_op jit(solution)/shard_map/all_to_all | solution.py:37
  34.1 0.1 reduce_sum.71
  34.2 10.3 %all-to-all-done = bf16[64,2,513]{2,1,0:T(2,128)(2,1)S(1)} async-done(((bf16[64,2,513]{2,1,0:T(2,128)(2,1)}), bf16[64,2,513]{2,1,0:T(2,128)(2,1)S(1)}, u32[]{:S(2)}, u32[]{:S(2)}) %all-to-all-start) | async-done | bytes 131360 | tf_op jit(solution)/shard_map/all_to_all | solution.py:37
  44.5 0.1 all_to_all.36
  44.6 0.1 convert_reduce_fusion.1
  44.8 0.1 convert_reduce_fusion.2
  44.9 0.1 fusion.8
  45.0 0.2 convolution_convert_fusion.1
  45.3 0.3 convolution_convert_fusion
  45.6 0.7 all_to_all.38
  46.3 5.5 %all-to-all-start.2 = ((bf16[64,2,512]{2,1,0:T(2,128)(2,1)}), bf16[64,2,512]{2,1,0:T(2,128)(2,1)S(1)}, u32[]{:S(2)}, u32[]{:S(2)}) async-start(bf16[64,2,512]{2,1,0:T(2,128)(2,1)} %all_to_all.38), calls=%async_computation.2 | async-start | bytes 262144 | tf_op jit(solution)/shard_map/all_to_all | solution.py:52
  51.8 10.0 %all-to-all-done.2 = bf16[64,2,512]{2,1,0:T(2,128)(2,1)S(1)} async-done(((bf16[64,2,512]{2,1,0:T(2,128)(2,1)}), bf16[64,2,512]{2,1,0:T(2,128)(2,1)S(1)}, u32[]{:S(2)}, u32[]{:S(2)}) %all-to-all-start.2) | async-done | bytes 131104 | tf_op jit(solution)/shard_map/all_to_all | solution.py:52
  61.8 0.1 all_to_all.40
  61.9 0.7 gather_fusion
  62.5 0.7 gather_fusion.1
  63.2 0.0 copy-done.3
  63.2 0.0 copy-done.4
  63.2 3.6 %fusion.1 = bf16[8192,256]{1,0:T(8,128)(2,1)S(1)} fusion(bf16[8192,256]{1,0:T(8,128)(2,1)} %param.6, f32[256]{0:T(256)S(1)} %copy-done.4, f32[64,256]{1,0:T(8,128)S(1)} %broadcast_multiply_fusion, f32[64,256]{1,0:T(8,128)S(1)} %gather_fusion), kind=kLoop, calls=%fused_computation.6 | loop fusion | flops 10485760 | bytes 8520704 | tf_op jit(solution)/shard_map/convert_element_type | solution.py:141
  66.8 0.0 copy-start.1
  66.8 53.4 %all_to_all.51 = bf16[4,2048,256]{2,1,0:T(8,128)(2,1)} all-to-all(bf16[4,2048,256]{2,1,0:T(8,128)(2,1)S(1)} %bitcast.45), channel_id=1, replica_groups=mesh['shuf'=64,'rep'=4] {'rep'}, dimensions={0} | all-to-all | bytes 8388608 | tf_op jit(solution)/shard_map/all_to_all | solution.py:145
  120.2 0.0 copy-done.1
  120.2 1.6 %broadcast_in_dim.11 = bf16[4,256,1024]{2,1,0:T(8,128)(2,1)} broadcast(bf16[256,1024]{1,0:T(8,128)(2,1)S(1)} %copy-done.1), dimensions={1,2} | broadcast | bytes 2621440 | tf_op jit(solution)/shard_map/broadcast_in_dim | solution.py:14
  121.8 3.8 %all-to-all-start.4 = ((bf16[4,256,1024]{2,1,0:T(8,128)(2,1)}), bf16[4,256,1024]{2,1,0:T(8,128)(2,1)S(1)}, u32[]{:S(2)}, u32[]{:S(2)}) async-start(bf16[4,256,1024]{2,1,0:T(8,128)(2,1)} %broadcast_in_dim.11), calls=%async_computation.4 | async-start | bytes 4194304 | tf_op jit(solution)/shard_map/all_to_all | solution.py:13
  125.6 6.2 %copy.14 = bf16[2048,4,256]{0,2,1:T(8,128)(2,1)} copy(bf16[2048,4,256]{2,0,1:T(8,128)(2,1)} %bitcast.44) | data formatting | bytes 8388608 | tf_op jit(solution)/shard_map/all_to_all | solution.py:145
  131.8 19.0 %all-to-all-done.4 = bf16[4,256,1024]{2,1,0:T(8,128)(2,1)S(1)} async-done(((bf16[4,256,1024]{2,1,0:T(8,128)(2,1)}), bf16[4,256,1024]{2,1,0:T(8,128)(2,1)S(1)}, u32[]{:S(2)}, u32[]{:S(2)}) %all-to-all-start.4) | async-done | bytes 2097184 | tf_op jit(solution)/shard_map/all_to_all | solution.py:13
  150.9 0.0 copy-start
  150.9 2.7 %fusion.10 = bf16[2048,1024]{1,0:T(8,128)(2,1)S(1)} fusion(bf16[2048,1024]{0,1:T(8,128)(2,1)} %bitcast.40, bf16[4,256,1024]{2,1,0:T(8,128)(2,1)S(1)} %all-to-all-done.4), kind=kOutput, calls=%fused_computation.25 | convolution fusion | flops 1073741824 | bytes 5767168 | tf_op jit(solution)/shard_map/dot_general | solution.py:149
  153.5 0.0 copy-done
  153.5 1.3 fusion.12
  154.8 1.3 fusion.14
  156.2 4.3 %add_convert_fusion = bf16[2048,1024]{1,0:T(8,128)(2,1)} fusion(bf16[2048,1024]{1,0:T(8,128)(2,1)S(1)} %fusion.10, bf16[2048,1024]{1,0:T(8,128)(2,1)S(1)} %fusion.12, bf16[2048,1024]{1,0:T(8,128)(2,1)S(1)} %fusion.14, bf16[2048,1024]{0,1:T(8,128)(2,1)S(1)} %bitcast.43, bf16[4,256,1024]{2,1,0:T(8,128)(2,1)S(1)} %all-to-all-done.4), kind=kOutput, calls=%fused_computation.14 | convolution fusion | flops 1092616192 | bytes 18350080 | tf_op jit(solution)/shard_map/dot_general | solution.py:149
  (11 shorter events, 0.1 us)
Async XLA Ops:
  0.0 20.5 %copy-start.5 = (s32[64]{0:T(128)S(1)}, s32[64]{0:T(128)}, u32[]{:S(2)}) copy-start(s32[64]{0:T(128)} %param.7) | copy-start | bytes 772
  0.0 20.5 %copy-start.2 = (s32[64,1]{0,1:T(1,128)S(1)}, s32[64,1]{0,1:T(1,128)}, u32[]{:S(2)}) copy-start(s32[64,1]{0,1:T(1,128)} %param.8) | copy-start | bytes 772
  4.1 21.8 %all-to-all-start.1 = ((f32[64,1,512]{2,1,0:T(1,128)}), f32[64,1,512]{2,1,0:T(1,128)S(1)}, u32[]{:S(2)}, u32[]{:S(2)}) async-start(f32[64,1,512]{2,1,0:T(1,128)} %broadcast_in_dim.10), calls=%async_computation.1 | async-start | bytes 262144 | tf_op jit(solution)/shard_map/all_to_all | solution.py:13
  15.8 47.4 %copy-start.3 = (f32[256]{0:T(256)S(1)}, f32[256]{0:T(256)}, u32[]{:S(2)}) copy-start(f32[256]{0:T(256)} %param.9) | copy-start | bytes 3076
  15.8 47.4 %copy-start.4 = (f32[256]{0:T(256)S(1)}, f32[256]{0:T(256)}, u32[]{:S(2)}) copy-start(f32[256]{0:T(256)} %param.10) | copy-start | bytes 3076
  25.9 18.7 %all-to-all-start = ((bf16[64,2,513]{2,1,0:T(2,128)(2,1)}), bf16[64,2,513]{2,1,0:T(2,128)(2,1)S(1)}, u32[]{:S(2)}, u32[]{:S(2)}) async-start(bf16[64,2,513]{2,1,0:T(2,128)(2,1)} %pad_maximum_fusion), calls=%async_computation | async-start | bytes 327680 | tf_op jit(solution)/shard_map/all_to_all | solution.py:37
  46.3 15.5 %all-to-all-start.2 = ((bf16[64,2,512]{2,1,0:T(2,128)(2,1)}), bf16[64,2,512]{2,1,0:T(2,128)(2,1)S(1)}, u32[]{:S(2)}, u32[]{:S(2)}) async-start(bf16[64,2,512]{2,1,0:T(2,128)(2,1)} %all_to_all.38), calls=%async_computation.2 | async-start | bytes 262144 | tf_op jit(solution)/shard_map/all_to_all | solution.py:52
  66.8 53.4 %copy-start.1 = (bf16[256,1024]{1,0:T(8,128)(2,1)S(1)}, bf16[256,1024]{1,0:T(8,128)(2,1)}, u32[]{:S(2)}) copy-start(bf16[256,1024]{1,0:T(8,128)(2,1)} %param.11) | copy-start | bytes 1572868
  121.8 29.0 %all-to-all-start.4 = ((bf16[4,256,1024]{2,1,0:T(8,128)(2,1)}), bf16[4,256,1024]{2,1,0:T(8,128)(2,1)S(1)}, u32[]{:S(2)}, u32[]{:S(2)}) async-start(bf16[4,256,1024]{2,1,0:T(8,128)(2,1)} %broadcast_in_dim.11), calls=%async_computation.4 | async-start | bytes 4194304 | tf_op jit(solution)/shard_map/all_to_all | solution.py:13
  150.9 2.7 %copy-start = (bf16[2048,4,256]{0,2,1:T(8,128)(2,1)S(1)}, bf16[2048,4,256]{0,2,1:T(8,128)(2,1)}, u32[]{:S(2)}) copy-start(bf16[2048,4,256]{0,2,1:T(8,128)(2,1)} %copy.14) | copy-start | bytes 12582916
where the time goes:
time: 161 us; the launch traced here: 160 us
  blocking collectives  53.4 us (33%)
  waiting for transfers between devices  41.5 us (26%)
  starting transfers between devices  29.2 us (18%)
  other arithmetic  14 us (9%)
  local copies, waits for them, and re-layouts  11.8 us (7%)
  matrix products  10.2 us (6%)
    all_to_all x1, blocking collectives, on_device(): lax.all_to_all(standard, 'rep', split_axis=0, concat_axis=1, tiled=True)  53.4 us
    all_to_all x2, waiting for transfers between devices, from_everyone(): lax.all_to_all(jnp.broadcast_to(value[None], (peers, *value.shape)), axis...  21.2 us
    all_to_all x2, starting transfers between devices, from_everyone(): lax.all_to_all(jnp.broadcast_to(value[None], (peers, *value.shape)), axis...  15.5 us
    all_to_all x1, waiting for transfers between devices, side_by_side(): lax.all_to_all(both, axis, split_axis=split_dim, concat_axis=concat_dim,...  10.3 us
    all_to_all x1, waiting for transfers between devices, in_one_piece(): lax.all_to_all(both, axis, split_axis=split_dim, concat_axis=concat_dim,...  10 us
    dot_general x4, matrix products, on_device(): jnp.dot(full_rows[:, block * local_cols:(block + 1) * local_cols], full_w...  9.54 us
    all_to_all x1, starting transfers between devices, side_by_side(): lax.all_to_all(both, axis, split_axis=split_dim, concat_axis=concat_dim,...  8.21 us
    all_to_all x1, local copies, waits for them, and re-layouts, on_device(): lax.all_to_all(standard, 'rep', split_axis=0, concat_axis=1, tiled=True)  6.2 us
  transfers between devices with their start and end apart: 4, of which 4 were waited for; matrix products, arithmetic and copies ran while one was open for 9% of the time, Pallas kernels for 0%

commit v1 on v0

--- a/solution.py
+++ b/solution.py
@@ -142,7 +142,11 @@
         jnp.bfloat16
     )
     standard = scored.reshape(local_rows, local_cols)
-    full_rows = lax.all_to_all(standard, "rep", split_axis=0, concat_axis=1, tiled=True)
+    current_arr = lax.axis_size("rep")
+    carry_out = jnp.split(standard, current_arr, 0)
+    local_now = jnp.stack(carry_out)
+    arr_now = lax.all_to_all(local_now, "rep", concat_axis=0, split_axis=0)
+    full_rows = jnp.concatenate(arr_now, 1)
     full_weight = gathered_copies(out_weight, "rep", 0)
     summed = jnp.zeros((full_rows.shape[0], full_weight.shape[1]), jnp.float32)
     for block in range(lax.axis_size("rep")):

time: 161 us -> 155 us (0.963)
  waiting for transfers between devices: 41.5 us -> 17.8 us
  local copies, waits for them, and re-layouts: 11.8 us -> 23.2 us
  other arithmetic: 14 us -> 22.7 us
    all_to_all x2, waiting for transfers between devices: 21.2 us -> 4.6 us  [from_everyone(): lax.all_to_all(jnp.broadcast_to(value[None], (peers, *value.shape)), axis...]
    another operation x0 -> x4, local copies, waits for them, and re-layouts: none -> 8.2 us  [on_device(): local_now = jnp.stack(carry_out)]
    all_to_all x1, waiting for transfers between devices: 10 us -> 2.91 us  [in_one_piece(): lax.all_to_all(both, axis, split_axis=split_dim, concat_axis=concat_dim,...]
    convert_element_type x0 -> x1, local copies, waits for them, and re-layouts: none -> 7.08 us  [on_device(): widened = shaped.astype(jnp.float32)]
    all_to_all x1 -> x0, local copies, waits for them, and re-layouts: 6.2 us -> none  [on_device(): lax.all_to_all(standard, 'rep', split_axis=0, concat_axis=1, tiled=True)]
    convert_element_type x1, other arithmetic: 3.55 us -> 8.4 us  [on_device(): ((widened - tile_center[:, None, :]) * tile_scale[:, None, :] + col_bias)...]
    another operation x0 -> x1, other arithmetic: none -> 3.79 us  [on_device(): local_now = jnp.stack(carry_out)]
    split x0 -> x1, local copies, waits for them, and re-layouts: none -> 2.11 us  [on_device(): carry_out = jnp.split(standard, current_arr, 0)]
  transfers between devices with their start and end apart: 4 -> 4, of which waited for: 4 -> 4; matrix products, arithmetic and copies ran while one was open for 9% -> 25% of each run, Pallas kernels for 0% -> 0%
where the time goes in v1:
time: 155 us
  blocking collectives  52 us (34%)
  starting transfers between devices  29.7 us (19%)
  local copies, waits for them, and re-layouts  23.2 us (15%)
  other arithmetic  22.7 us (15%)
  waiting for transfers between devices  17.8 us (11%)
  matrix products  8.84 us (6%)
    all_to_all x1, blocking collectives, on_device(): arr_now = lax.all_to_all(local_now, 'rep', concat_axis=0, split_axis=0)  52 us
    all_to_all x2, starting transfers between devices, from_everyone(): lax.all_to_all(jnp.broadcast_to(value[None], (peers, *value.shape)), axis...  16.1 us
    all_to_all x1, waiting for transfers between devices, side_by_side(): lax.all_to_all(both, axis, split_axis=split_dim, concat_axis=concat_dim,...  10.3 us
    convert_element_type x1, other arithmetic, on_device(): ((widened - tile_center[:, None, :]) * tile_scale[:, None, :] + col_bias)...  8.4 us
    another operation x4, local copies, waits for them, and re-layouts, on_device(): local_now = jnp.stack(carry_out)  8.2 us
    dot_general x4, matrix products, on_device(): jnp.dot(full_rows[:, block * local_cols:(block + 1) * local_cols], full_w...  8.19 us
    all_to_all x1, starting transfers between devices, side_by_side(): lax.all_to_all(both, axis, split_axis=split_dim, concat_axis=concat_dim,...  8.19 us
    convert_element_type x1, local copies, waits for them, and re-layouts, on_device(): widened = shaped.astype(jnp.float32)  7.08 us
  transfers between devices with their start and end apart: 4, of which 4 were waited for; matrix products, arithmetic and copies ran while one was open for 25% of the time, Pallas kernels for 0%

profile of v1, /device:TPU:32, one launch (start us, length us, event | category | flops | bytes accessed | tf_op | source)
XLA Modules:
  0.0 154.5 jit_solution(16578201030681381784)
XLA Ops:
  0.0 0.0 copy-start.4
  0.0 0.0 copy-start.1
  0.0 3.3 %convert_reduce_fusion = (f32[256]{0:T(256)S(1)}, f32[256]{0:T(256)S(1)}) fusion(bf16[8192,256]{1,0:T(8,128)(2,1)} %param.6), kind=kLoop, calls=%fused_computation.9 | loop fusion | flops 8388096 | bytes 4196352 | tf_op jit(solution)/shard_map/reduce_sum | solution.py:93
  3.4 0.7 broadcast_in_dim.10
  4.1 11.8 %all-to-all-start.1 = ((f32[64,1,512]{2,1,0:T(1,128)}), f32[64,1,512]{2,1,0:T(1,128)S(1)}, u32[]{:S(2)}, u32[]{:S(2)}) async-start(f32[64,1,512]{2,1,0:T(1,128)} %broadcast_in_dim.10), calls=%async_computation.1 | async-start | bytes 262144 | tf_op jit(solution)/shard_map/all_to_all | solution.py:13
  15.8 4.6 %bitcast_reduce_fusion = (f32[64,256]{1,0:T(8,128)S(1)}, f32[64,256]{1,0:T(8,128)S(1)}) fusion(bf16[8192,256]{1,0:T(8,128)(2,1)} %param.6), kind=kLoop, calls=%fused_computation.65 | loop fusion | flops 8355840 | bytes 4325376 | tf_op jit(solution)/shard_map/reduce_sum | solution.py:91
  20.5 0.0 copy-done.4
  20.5 0.0 copy-done.1
  20.5 0.1 fusion.21
  20.6 0.1 reduce_window_sum.11
  20.7 0.2 select_reduce_fusion
  20.9 0.8 scatter_custom_fusion.1
  21.7 0.2 concatenate.23
  21.9 0.9 scatter_custom_fusion
  22.8 0.1 concatenate.18
  22.9 0.8 pad_maximum_fusion.1
  23.7 2.1 %all-to-all-done.1 = f32[64,1,512]{2,1,0:T(1,128)S(1)} async-done(((f32[64,1,512]{2,1,0:T(1,128)}), f32[64,1,512]{2,1,0:T(1,128)S(1)}, u32[]{:S(2)}, u32[]{:S(2)}) %all-to-all-start.1) | async-done | bytes 131104 | tf_op jit(solution)/shard_map/all_to_all | solution.py:13
  25.9 8.2 %all-to-all-start = ((bf16[64,2,513]{2,1,0:T(2,128)(2,1)}), bf16[64,2,513]{2,1,0:T(2,128)(2,1)S(1)}, u32[]{:S(2)}, u32[]{:S(2)}) async-start(bf16[64,2,513]{2,1,0:T(2,128)(2,1)} %pad_maximum_fusion.1), calls=%async_computation | async-start | bytes 327680 | tf_op jit(solution)/shard_map/all_to_all | solution.py:37
  34.0 0.1 reduce_sum.71
  34.2 10.3 %all-to-all-done = bf16[64,2,513]{2,1,0:T(2,128)(2,1)S(1)} async-done(((bf16[64,2,513]{2,1,0:T(2,128)(2,1)}), bf16[64,2,513]{2,1,0:T(2,128)(2,1)S(1)}, u32[]{:S(2)}, u32[]{:S(2)}) %all-to-all-start) | async-done | bytes 131360 | tf_op jit(solution)/shard_map/all_to_all | solution.py:37
  44.5 0.1 all_to_all.25
  44.6 0.1 convert_reduce_fusion.1
  44.7 0.1 convert_reduce_fusion.2
  44.9 0.1 fusion.4
  45.0 0.2 convolution_convert_fusion.1
  45.2 0.3 convolution_convert_fusion
  45.5 0.7 all_to_all.27
  46.3 5.5 %all-to-all-start.2 = ((bf16[64,2,512]{2,1,0:T(2,128)(2,1)}), bf16[64,2,512]{2,1,0:T(2,128)(2,1)S(1)}, u32[]{:S(2)}, u32[]{:S(2)}) async-start(bf16[64,2,512]{2,1,0:T(2,128)(2,1)} %all_to_all.27), calls=%async_computation.2 | async-start | bytes 262144 | tf_op jit(solution)/shard_map/all_to_all | solution.py:52
  51.7 0.0 copy-start
  51.7 7.1 %copy.22 = f32[64,128,256]{1,0,2:T(8,128)} copy(bf16[64,128,256]{2,1,0:T(8,128)(2,1)} %bitcast.37) | data formatting | bytes 12582912 | tf_op jit(solution)/shard_map/convert_element_type | solution.py:90
  58.8 0.0 copy-start.2
  58.8 0.0 copy-start.3
  58.8 2.9 %all-to-all-done.2 = bf16[64,2,512]{2,1,0:T(2,128)(2,1)S(1)} async-done(((bf16[64,2,512]{2,1,0:T(2,128)(2,1)}), bf16[64,2,512]{2,1,0:T(2,128)(2,1)S(1)}, u32[]{:S(2)}, u32[]{:S(2)}) %all-to-all-start.2) | async-done | bytes 131104 | tf_op jit(solution)/shard_map/all_to_all | solution.py:52
  61.8 0.0 copy-done
  61.8 1.7 %broadcast_in_dim.11 = bf16[4,256,1024]{2,1,0:T(8,128)(2,1)} broadcast(bf16[256,1024]{1,0:T(8,128)(2,1)S(1)} %copy-done), dimensions={1,2} | broadcast | bytes 2621440 | tf_op jit(solution)/shard_map/broadcast_in_dim | solution.py:14
  63.4 4.3 %all-to-all-start.4 = ((bf16[4,256,1024]{2,1,0:T(8,128)(2,1)}), bf16[4,256,1024]{2,1,0:T(8,128)(2,1)S(1)}, u32[]{:S(2)}, u32[]{:S(2)}) async-start(bf16[4,256,1024]{2,1,0:T(8,128)(2,1)} %broadcast_in_dim.11), calls=%async_computation.4 | async-start | bytes 4194304 | tf_op jit(solution)/shard_map/all_to_all | solution.py:13
  67.7 0.1 all_to_all.29
  67.8 0.7 gather_fusion
  68.5 0.7 gather_fusion.1
  69.1 0.0 copy-done.2
  69.1 0.1 copy.23
  69.2 0.1 copy.21
  69.3 0.0 copy-done.3
  69.3 8.4 %add_convert_fusion.1 = bf16[64,128,256]{1,0,2:T(8,128)(2,1)S(1)} fusion(f32[64,128,256]{1,0,2:T(8,128)} %copy.22, f32[256]{0:T(256)S(1)} %copy-done.3, f32[64,256]{0,1:T(8,128)S(1)} %copy.23, f32[64,256]{0,1:T(8,128)S(1)} %copy.21), kind=kLoop, calls=%fused_computation.5 | loop fusion | flops 8388608 | bytes 12715008 | tf_op jit(solution)/shard_map/convert_element_type | solution.py:141
  77.8 2.1 %fusion.33 = (bf16[16,128,256]{1,0,2:T(8,128)(2,1)}, bf16[16,128,256]{1,0,2:T(8,128)(2,1)}, bf16[16,128,256]{1,0,2:T(8,128)(2,1)}, bf16[16,128,256]{1,0,2:T(8,128)(2,1)S(1)}) fusion(bf16[64,128,256]{1,0,2:T(8,128)(2,1)S(1)} %add_convert_fusion.1), kind=kLoop, calls=%fused_computation.67 | loop fusion | bytes 8388608 | tf_op jit(solution)/shard_map/split | solution.py:146
  79.9 2.3 %stack.15 = bf16[1,2048,256]{1,2,0:T(8,128)(2,1)} reshape(bf16[16,128,256]{1,0,2:T(8,128)(2,1)} %get-tuple-element.9) | data formatting | bytes 2097152 | tf_op jit(solution)/shard_map/stack | solution.py:147
  82.2 2.3 %stack.18 = bf16[1,2048,256]{1,2,0:T(8,128)(2,1)} reshape(bf16[16,128,256]{1,0,2:T(8,128)(2,1)} %get-tuple-element.10) | data formatting | bytes 2097152 | tf_op jit(solution)/shard_map/stack | solution.py:147
  84.5 2.3 %stack.17 = bf16[1,2048,256]{1,2,0:T(8,128)(2,1)} reshape(bf16[16,128,256]{1,0,2:T(8,128)(2,1)} %get-tuple-element.11) | data formatting | bytes 2097152 | tf_op jit(solution)/shard_map/stack | solution.py:147
  86.8 1.3 stack.16
  88.1 3.8 %pad_maximum_fusion = bf16[4,2048,256]{1,2,0:T(8,128)(2,1)} fusion(bf16[1,2048,256]{1,2,0:T(8,128)(2,1)} %stack.18, bf16[1,2048,256]{1,2,0:T(8,128)(2,1)} %stack.17, bf16[1,2048,256]{1,2,0:T(8,128)(2,1)} %stack.16, bf16[1,2048,256]{1,2,0:T(8,128)(2,1)} %stack.15), kind=kLoop, calls=%fused_computation.8 | loop fusion | flops 6291456 | bytes 8388608 | tf_op jit(solution)/shard_map/stack | solution.py:147
  91.9 2.5 %all-to-all-done.4 = bf16[4,256,1024]{2,1,0:T(8,128)(2,1)S(1)} async-done(((bf16[4,256,1024]{2,1,0:T(8,128)(2,1)}), bf16[4,256,1024]{2,1,0:T(8,128)(2,1)S(1)}, u32[]{:S(2)}, u32[]{:S(2)}) %all-to-all-start.4) | async-done | bytes 2097184 | tf_op jit(solution)/shard_map/all_to_all | solution.py:13
  94.3 52.0 %all_to_all.37 = bf16[4,2048,256]{1,2,0:T(8,128)(2,1)S(1)} all-to-all(bf16[4,2048,256]{1,2,0:T(8,128)(2,1)} %pad_maximum_fusion), channel_id=1, replica_groups=mesh['shuf'=64,'rep'=4] {'rep'}, dimensions={0} | all-to-all | bytes 8388608 | tf_op jit(solution)/shard_map/all_to_all | solution.py:148
  146.3 1.3 fusion.6
  147.6 1.3 fusion.8
  148.9 1.3 fusion.10
  150.2 4.3 %add_convert_fusion = bf16[2048,1024]{1,0:T(8,128)(2,1)} fusion(bf16[2048,1024]{1,0:T(8,128)(2,1)S(1)} %fusion.6, bf16[2048,1024]{1,0:T(8,128)(2,1)S(1)} %fusion.8, bf16[2048,1024]{1,0:T(8,128)(2,1)S(1)} %fusion.10, bf16[2048,1024]{0,1:T(8,128)(2,1)S(1)} %bitcast.41, bf16[4,256,1024]{2,1,0:T(8,128)(2,1)S(1)} %all-to-all-done.4), kind=kOutput, calls=%fused_computation.4 | convolution fusion | flops 1092616192 | bytes 18350080 | tf_op jit(solution)/shard_map/dot_general | solution.py:153
  (11 shorter events, 0.1 us)
Async XLA Ops:
  0.0 20.5 %copy-start.4 = (s32[64]{0:T(128)S(1)}, s32[64]{0:T(128)}, u32[]{:S(2)}) copy-start(s32[64]{0:T(128)} %param.7) | copy-start | bytes 772
  0.0 20.5 %copy-start.1 = (s32[64,1]{0,1:T(1,128)S(1)}, s32[64,1]{0,1:T(1,128)}, u32[]{:S(2)}) copy-start(s32[64,1]{0,1:T(1,128)} %param.8) | copy-start | bytes 772
  4.1 21.8 %all-to-all-start.1 = ((f32[64,1,512]{2,1,0:T(1,128)}), f32[64,1,512]{2,1,0:T(1,128)S(1)}, u32[]{:S(2)}, u32[]{:S(2)}) async-start(f32[64,1,512]{2,1,0:T(1,128)} %broadcast_in_dim.10), calls=%async_computation.1 | async-start | bytes 262144 | tf_op jit(solution)/shard_map/all_to_all | solution.py:13
  25.9 18.6 %all-to-all-start = ((bf16[64,2,513]{2,1,0:T(2,128)(2,1)}), bf16[64,2,513]{2,1,0:T(2,128)(2,1)S(1)}, u32[]{:S(2)}, u32[]{:S(2)}) async-start(bf16[64,2,513]{2,1,0:T(2,128)(2,1)} %pad_maximum_fusion.1), calls=%async_computation | async-start | bytes 327680 | tf_op jit(solution)/shard_map/all_to_all | solution.py:37
  46.3 15.5 %all-to-all-start.2 = ((bf16[64,2,512]{2,1,0:T(2,128)(2,1)}), bf16[64,2,512]{2,1,0:T(2,128)(2,1)S(1)}, u32[]{:S(2)}, u32[]{:S(2)}) async-start(bf16[64,2,512]{2,1,0:T(2,128)(2,1)} %all_to_all.27), calls=%async_computation.2 | async-start | bytes 262144 | tf_op jit(solution)/shard_map/all_to_all | solution.py:52
  51.7 10.0 %copy-start = (bf16[256,1024]{1,0:T(8,128)(2,1)S(1)}, bf16[256,1024]{1,0:T(8,128)(2,1)}, u32[]{:S(2)}) copy-start(bf16[256,1024]{1,0:T(8,128)(2,1)} %param.11) | copy-start | bytes 1572868
  58.8 10.3 %copy-start.2 = (f32[256]{0:T(256)S(1)}, f32[256]{0:T(256)}, u32[]{:S(2)}) copy-start(f32[256]{0:T(256)} %param.9) | copy-start | bytes 3076
  58.8 10.5 %copy-start.3 = (f32[256]{0:T(256)S(1)}, f32[256]{0:T(256)}, u32[]{:S(2)}) copy-start(f32[256]{0:T(256)} %param.10) | copy-start | bytes 3076
  63.4 30.9 %all-to-all-start.4 = ((bf16[4,256,1024]{2,1,0:T(8,128)(2,1)}), bf16[4,256,1024]{2,1,0:T(8,128)(2,1)S(1)}, u32[]{:S(2)}, u32[]{:S(2)}) async-start(bf16[4,256,1024]{2,1,0:T(8,128)(2,1)} %broadcast_in_dim.11), calls=%async_computation.4 | async-start | bytes 4194304 | tf_op jit(solution)/shard_map/all_to_all | solution.py:13
